TPU v7x, 32 devices: a whole 2x2x4 slice. The times are simulated.
32 devices in a mesh: row: 16 (over z, y, x), col: 2 (over core).
Axes of the slice: x: 2, y: 2, z: 4, core: 2. Of those that a mesh axis runs over, the one named last changes fastest.
Arguments:
- messages: float32 [32, 16, 2, 16, 128], P(('row', 'col')), may hold values from -6 to 6
- dst_local: int32 [32, 16, 2, 16], P(('row', 'col')), may hold values from 0 to 255
- counts: int32 [32, 16, 2], P(('row', 'col')), may hold values from 8 to 16, as said below
- degrees: int32 [8192], P(('row', 'col')), may hold values from 1 to 8
Outputs:
- aggregate: float32 [8192, 128], P(('row', 'col'))
Inputs may be any that keep to these rules, and one draw needn't show every extreme that they name: For every sender and group, the counts over the group's 2 ranges sum to exactly 24. In each group one range receives 16 live slots from every sender.
All inputs are finite; a program needn't handle non-finite values.
Results may differ from a plain program's by a relative error of at most 0.0003.
Values sent between devices are 32-bit elements; how exact they have to be, the bound alone decides.
A program may use at most 64 MiB of HBM per device.

v0:
```python
import jax
import jax.numpy as jnp
from jax import lax
from jax.sharding import PartitionSpec as P


def body(messages, dst_local, counts, degrees):
    slots = messages.shape[3]
    width = messages.shape[4]
    owned = degrees.shape[0]
    slot_index = lax.broadcasted_iota(jnp.int32, counts.shape + (slots,), 3)
    alive_int = (slot_index < counts[..., None]).astype(jnp.int32)
    alive_mask = alive_int.astype(jnp.float32)
    masked = messages * alive_mask[..., None]
    received, labels = (
        lax.all_to_all(
            lax.all_to_all(masked, "row", split_axis=1, concat_axis=0, tiled=True),
            "col",
            split_axis=2,
            concat_axis=1,
            tiled=True,
        ),
        lax.all_to_all(
            lax.all_to_all(dst_local, "row", split_axis=1, concat_axis=0, tiled=True),
            "col",
            split_axis=2,
            concat_axis=1,
            tiled=True,
        ),
    )
    summed = jax.ops.segment_sum(
        received.reshape(-1, width), labels.reshape(-1), num_segments=owned
    )
    scale = jnp.maximum(degrees, 1).astype(jnp.float32)
    return summed / scale[:, None]


def solution(mesh):
    in_specs = (
        P(("row", "col"), None, None, None, None),
        P(("row", "col"), None, None, None),
        P(("row", "col"), None, None),
        P(("row", "col")),
    )
    out_specs = P(("row", "col"), None)
    return jax.shard_map(body, mesh=mesh, in_specs=in_specs, out_specs=out_specs, check_vma=False)
```

profile of v0, /device:TPU:0, one launch (start us, length us, event | category | flops | bytes accessed | tf_op | source)
XLA Modules:
  0.0 40.6 jit_solution(9112248974094976545)
XLA Ops:
  0.0 8.3 %all-to-all-start = ((s32[1,16,2,16]{3,2,0,1:T(2,128)}), s32[1,16,2,16]{3,2,0,1:T(2,128)S(1)}, u32[]{:S(2)}, u32[]{:S(2)}) async-start(s32[1,16,2,16]{3,2,0,1:T(2,128)} %bitcast.18), calls=%async_computation | async-start | bytes 32768 | tf_op jit(solution)/shard_map/all_to_all | solution.py:24
  8.3 0.0 copy-start
  8.4 0.7 %copy-done = s32[1,16,2]{1,2,0:T(2,128)S(1)} copy-done((s32[1,16,2]{1,2,0:T(2,128)S(1)}, s32[1,16,2]{1,2,0:T(2,128)}, u32[]{:S(2)}) %copy-start) | copy-done | bytes 152
  9.0 0.1 copy.15
  9.1 0.1 fusion.2
  9.2 1.8 %bitcast_multiply_fusion = f32[1,16,2,16,128]{4,3,2,0,1:T(8,128)} fusion(f32[1,16,2,16,128]{4,3,2,1,0:T(8,128)} %param.4, f32[16,2,16]{2,1,0:T(2,128)S(1)} %fusion.2), kind=kLoop, calls=%fused_computation.1 | loop fusion | flops 65536 | bytes 526336 | tf_op jit(solution)/shard_map/mul | solution.py:14
  11.0 4.7 %all-to-all-done = s32[1,16,2,16]{3,2,0,1:T(2,128)S(1)} async-done(((s32[1,16,2,16]{3,2,0,1:T(2,128)}), s32[1,16,2,16]{3,2,0,1:T(2,128)S(1)}, u32[]{:S(2)}, u32[]{:S(2)}) %all-to-all-start) | async-done | bytes 2080 | tf_op jit(solution)/shard_map/all_to_all | solution.py:24
  15.7 0.1 reshape.45
  15.8 3.7 %all_to_all.42 = s32[2,1,256]{2,1,0:T(1,128)S(1)} all-to-all(s32[2,1,256]{2,1,0:T(1,128)S(1)} %reshape.45), channel_id=1, replica_groups=mesh['row'=16,'col'=2] {'col'}, dimensions={0} | all-to-all | bytes 4096 | tf_op jit(solution)/shard_map/all_to_all | solution.py:23
  19.5 0.0 copy-start.1
  19.5 3.7 %all-to-all-start.2 = ((f32[1,16,2,16,128]{4,3,2,0,1:T(8,128)}), f32[1,16,2,16,128]{4,3,2,0,1:T(8,128)S(1)}, u32[]{:S(2)}, u32[]{:S(2)}) async-start(f32[1,16,2,16,128]{4,3,2,0,1:T(8,128)} %bitcast_multiply_fusion), calls=%async_computation.2 | async-start | bytes 524288 | tf_op jit(solution)/shard_map/all_to_all | solution.py:17
  23.1 0.0 copy-done.1
  23.2 0.5 %broadcast.9 = s32[]{:T(128)} broadcast(s32[]{:T(128)} %constant.8), dimensions={} | broadcast | bytes 8 | tf_op jit(solution)/shard_map/all_to_all | solution.py:23
  23.7 0.7 %reduce = s32[2,256]{1,0:T(2,128)S(1)} reduce(s32[2,1,256]{2,1,0:T(1,128)S(1)} %all_to_all.42, s32[]{:T(128)} %broadcast.9), dimensions={1}, to_apply=%all_to_all.14.reduce_sub_computation | reduce | bytes 4100 | tf_op jit(solution)/shard_map/all_to_all | solution.py:23
  24.3 0.1 reshape.46
  24.4 0.1 reshape.36
  24.5 9.0 %all-to-all-done.2 = f32[1,16,2,16,128]{4,3,2,0,1:T(8,128)S(1)} async-done(((f32[1,16,2,16,128]{4,3,2,0,1:T(8,128)}), f32[1,16,2,16,128]{4,3,2,0,1:T(8,128)S(1)}, u32[]{:S(2)}, u32[]{:S(2)}) %all-to-all-start.2) | async-done | bytes 262176 | tf_op jit(solution)/shard_map/all_to_all | solution.py:17
  33.6 3.9 %all_to_all.43 = f32[16,1,2,16,128]{4,3,0,1,2:T(8,128)S(1)} all-to-all(f32[16,1,2,16,128]{4,3,0,1,2:T(8,128)S(1)} %copy.17), channel_id=1, replica_groups=mesh['row'=16,'col'=2] {'col'}, dimensions={2} | all-to-all | bytes 524288 | tf_op jit(solution)/shard_map/all_to_all | solution.py:16
  37.5 2.3 %scatter_custom_fusion = f32[256,128]{1,0:T(8,128)S(1)} fusion(s32[512]{0:T(512)S(1)} %reshape.36, f32[512,128]{1,0:T(8,128)S(1)} %bitcast.14, f32[]{:T(128)} %constant.0.clone.1), kind=kCustom, calls=%fused_computation.3 | custom fusion | flops 65536 | bytes 131076 | tf_op jit(solution)/shard_map/scatter-add | solution.py:31
  39.8 0.8 %broadcast_divide_fusion = f32[256,128]{1,0:T(8,128)} fusion(f32[256,128]{1,0:T(8,128)S(1)} %scatter_custom_fusion, f32[256]{0:T(256)S(1)} %maximum_convert_fusion), kind=kLoop, calls=%fused_computation.2 | loop fusion | flops 32768 | bytes 263168 | tf_op jit(solution)/shard_map/div | solution.py:35
  (5 shorter events, 0.1 us)
Async XLA Ops:
  0.0 15.7 %all-to-all-start = ((s32[1,16,2,16]{3,2,0,1:T(2,128)}), s32[1,16,2,16]{3,2,0,1:T(2,128)S(1)}, u32[]{:S(2)}, u32[]{:S(2)}) async-start(s32[1,16,2,16]{3,2,0,1:T(2,128)} %bitcast.18), calls=%async_computation | async-start | bytes 32768 | tf_op jit(solution)/shard_map/all_to_all | solution.py:24
  8.3 0.7 %copy-start = (s32[1,16,2]{1,2,0:T(2,128)S(1)}, s32[1,16,2]{1,2,0:T(2,128)}, u32[]{:S(2)}) copy-start(s32[1,16,2]{1,2,0:T(2,128)} %param.6) | copy-start | bytes 388
  19.5 3.7 %copy-start.1 = (s32[256]{0:T(256)S(1)}, s32[256]{0:T(256)}, u32[]{:S(2)}) copy-start(s32[256]{0:T(256)} %param.7) | copy-start | bytes 3076
  19.5 14.1 %all-to-all-start.2 = ((f32[1,16,2,16,128]{4,3,2,0,1:T(8,128)}), f32[1,16,2,16,128]{4,3,2,0,1:T(8,128)S(1)}, u32[]{:S(2)}, u32[]{:S(2)}) async-start(f32[1,16,2,16,128]{4,3,2,0,1:T(8,128)} %bitcast_multiply_fusion), calls=%async_computation.2 | async-start | bytes 524288 | tf_op jit(solution)/shard_map/all_to_all | solution.py:17
where the time goes:
time: 41 us; the launch traced here: 40.6 us
  waiting for transfers between devices  13.7 us (33%)
  starting transfers between devices  12 us (29%)
  blocking collectives  7.63 us (19%)
  other arithmetic  5.57 us (14%)
  local copies, waits for them, and re-layouts  1.57 us (4%)
    all_to_all x1, waiting for transfers between devices, body(): lax.all_to_all(masked, 'row', split_axis=1, concat_axis=0, tiled=True)  9.04 us
    all_to_all x1, starting transfers between devices, body(): lax.all_to_all(dst_local, 'row', split_axis=1, concat_axis=0, tiled=True)  8.34 us
    all_to_all x1, waiting for transfers between devices, body(): lax.all_to_all(dst_local, 'row', split_axis=1, concat_axis=0, tiled=True)  4.7 us
    all_to_all x1, blocking collectives, body(): lax.all_to_all(lax.all_to_all(masked, 'row', split_axis=1, concat_axis=0,...  3.94 us
    all_to_all x1, blocking collectives, body(): lax.all_to_all(lax.all_to_all(dst_local, 'row', split_axis=1, concat_axis...  3.69 us
    all_to_all x1, starting transfers between devices, body(): lax.all_to_all(masked, 'row', split_axis=1, concat_axis=0, tiled=True)  3.66 us
    scatter-add x1, other arithmetic, body(): jax.ops.segment_sum(received.reshape(-1, width), labels.reshape(-1), num_...  2.28 us
    mul x1, other arithmetic, body(): masked = messages * alive_mask[..., None]  1.78 us
  transfers between devices with their start and end apart: 2, of which 2 were waited for; matrix products, arithmetic and copies ran while one was open for 8% of the time, Pallas kernels for 0%

commit v1 on v0

v1 whole, which is shorter than its diff:
```python
import functools

import jax
import jax.numpy as jnp
from jax import lax
from jax.experimental import pallas as pl
from jax.experimental.pallas import tpu as pltpu
from jax.sharding import PartitionSpec as P

MESH = pl.DeviceIdType.MESH
LANES = 128


def exchange(rows, cols, msg_ref, dst_ref, cnt_ref, out_ref, stage, recv, labels, copy_sem, send_sem, recv_sem):
    slots = msg_ref.shape[1]
    owned = out_ref.shape[0]
    total = rows * cols
    pack = LANES // slots
    planes = total // pack
    half = max(planes // 2, 1)
    me = lax.axis_index("row") * cols + lax.axis_index("col")
    plane, seat = me // pack, me % pack
    side = plane // half
    mirrored = plane * (1 - side) + (planes - 1 - plane) * side

    load = pltpu.make_async_copy(msg_ref, stage.at[:, pl.ds(0, slots), :], copy_sem.at[0])
    load.start()

    def partner(step, j):
        if planes > 1:
            ahead = planes - 1 - step if step < half else (mirrored + planes - 1 - step) % half
            there = ahead * (1 - side) + (planes - 1 - ahead) * side
        else:
            there = 0
        return there * pack + (seat + j) % pack

    def each(visit):
        for step in range(planes):
            first = 1 if step == planes - 1 else 0
            if total <= 64:
                for j in range(first, pack):
                    visit(partner(step, j))
            else:
                lax.fori_loop(first, pack, lambda j, c, step=step: (visit(partner(step, j)), c)[1], 0)

    barrier = pltpu.get_barrier_semaphore()
    each(lambda t: pl.semaphore_signal(barrier, inc=1, device_id=(t // cols, t % cols), device_id_type=MESH))

    lane = lax.broadcasted_iota(jnp.int32, (cols, slots), 1)
    row = lax.broadcasted_iota(jnp.int32, (cols, slots), 0)
    labels[...] = jnp.zeros_like(labels)
    for g in range(rows):
        live = jnp.zeros((cols, slots), jnp.int32)
        for c in range(cols):
            live = jnp.where(row == c, cnt_ref[c, g], live)
        value = jnp.where(lane < live, dst_ref[0, g], -1)
        labels[pl.ds(g * cols, cols), pl.ds(0, slots)] = value.astype(jnp.float32)
    rolled = pltpu.roll(labels[...], seat * slots, 1)
    stage[:, slots, :] = rolled
    load.wait()
    own = pltpu.make_async_copy(stage.at[me], recv.at[me], recv_sem.at[plane])

    pl.semaphore_wait(barrier, total - 1)

    def send(t):
        pltpu.make_async_remote_copy(
            src_ref=stage.at[t],
            dst_ref=recv.at[me],
            send_sem=send_sem,
            recv_sem=recv_sem.at[plane],
            device_id=(t // cols, t % cols),
            device_id_type=MESH,
        ).start()

    each(send)
    own.start()

    vertex = lax.broadcasted_iota(jnp.int32, (owned, LANES), 0).astype(jnp.float32)
    width = msg_ref.shape[2]

    def block(q, acc):
        part = recv.at[pl.ds(q * pack, pack)]
        pltpu.make_async_copy(part, part, recv_sem.at[q]).wait()
        label = jnp.sum(recv[pl.ds(q * pack, pack), slots, :], axis=0, keepdims=True)
        hot = (vertex == label).astype(jnp.bfloat16)
        values = recv[pl.ds(q * pack, pack), pl.ds(0, slots), :].reshape(pack * slots, width)
        high = values.astype(jnp.bfloat16)
        low = (values - high.astype(jnp.float32)).astype(jnp.bfloat16)
        both = jnp.concatenate([high, low], axis=1)
        return acc + jnp.dot(hot, both, preferred_element_type=jnp.float32)

    acc = jnp.zeros((owned, 2 * width), jnp.float32)
    if planes <= 8:
        for d in range(planes):
            acc = block((plane + d) % planes, acc)
    else:
        acc = lax.fori_loop(0, planes, lambda d, a: block((plane + d) % planes, a), acc)
    out_ref[...] = acc[:, :width] + acc[:, width:]
    sent = stage.at[pl.ds(0, total - 1)]
    pltpu.make_async_copy(sent, sent, send_sem).wait()


def solution(mesh):
    rows, cols = mesh.shape["row"], mesh.shape["col"]
    total = rows * cols

    def body(messages, dst_local, counts, degrees):
        slots, width = messages.shape[3:]
        owned = degrees.shape[0]
        planes = total // (LANES // slots)
        summed = pl.pallas_call(
            functools.partial(exchange, rows, cols),
            out_shape=jax.ShapeDtypeStruct((owned, width), jnp.float32),
            in_specs=[
                pl.BlockSpec(memory_space=pl.ANY),
                pl.BlockSpec(memory_space=pltpu.VMEM),
                pl.BlockSpec(memory_space=pltpu.SMEM),
            ],
            out_specs=pl.BlockSpec(memory_space=pltpu.VMEM),
            scratch_shapes=[
                pltpu.VMEM((total, slots + 1, width), jnp.float32),
                pltpu.VMEM((total, slots + 1, width), jnp.float32),
                pltpu.VMEM((total, LANES), jnp.float32),
                pltpu.SemaphoreType.DMA((1,)),
                pltpu.SemaphoreType.DMA,
                pltpu.SemaphoreType.DMA((planes,)),
            ],
            compiler_params=pltpu.CompilerParams(collective_id=0, has_side_effects=True),
        )(messages.reshape(total, slots, width), dst_local, counts[0].T)
        scale = jnp.maximum(degrees, 1).astype(jnp.float32)
        return summed / scale[:, None]

    in_specs = (
        P(("row", "col"), None, None, None, None),
        P(("row", "col"), None, None, None),
        P(("row", "col"), None, None),
        P(("row", "col")),
    )
    return jax.shard_map(body, mesh=mesh, in_specs=in_specs, out_specs=P(("row", "col"), None), check_vma=False)
```

time: 41 us -> 17.7 us (0.43)
  Pallas kernels: 0 us -> 15.1 us
  waiting for transfers between devices: 13.7 us -> 0 us
  starting transfers between devices: 12 us -> 0 us
  blocking collectives: 7.63 us -> 0 us
  other arithmetic: 5.57 us -> 1.67 us
  local copies, waits for them, and re-layouts: 1.57 us -> 0.68 us
    pallas_call x0 -> x1, Pallas kernels: none -> 15.1 us  [body(): pl.pallas_call(functools.partial(exchange, rows, cols), out_shape=jax.Sha...]
    all_to_all x2 -> x0, waiting for transfers between devices: 13.7 us -> none  [the longest x1 9.04 us: body(): lax.all_to_all(masked, 'row', split_axis=1, concat_axis=0, tiled=True)]
    all_to_all x2 -> x0, starting transfers between devices: 12 us -> none  [the longest x1 8.34 us: body(): lax.all_to_all(dst_local, 'row', split_axis=1, concat_axis=0, tiled=True)]
    all_to_all x2 -> x0, blocking collectives: 7.63 us -> none  [the longest x1 3.94 us: body(): lax.all_to_all(lax.all_to_all(masked, 'row', split_axis=1, concat_axis=0,...]
    scatter-add x1 -> x0, other arithmetic: 2.28 us -> none  [body(): jax.ops.segment_sum(received.reshape(-1, width), labels.reshape(-1), num_...]
    mul x1 -> x0, other arithmetic: 1.78 us -> none  [body(): masked = messages * alive_mask[..., None]]
    div x1, other arithmetic: 0.76 us -> 1.67 us  [body(): return summed / scale[:, None]]
    all_to_all x1 -> x0, other arithmetic: 0.66 us -> none  [body(): lax.all_to_all(lax.all_to_all(dst_local, 'row', split_axis=1, concat_axis...]
  transfers between devices with their start and end apart: 2 -> 0, of which waited for: 2 -> 0; matrix products, arithmetic and copies ran while one was open for 8% -> 0% of each run, Pallas kernels for 0% -> 0%
where the time goes in v1:
time: 17.7 us; the launch traced here: 17.5 us
  Pallas kernels  15.1 us (85%)
  other arithmetic  1.67 us (9%)
  local copies, waits for them, and re-layouts  0.68 us (4%)
    pallas_call x1, Pallas kernels, body(): pl.pallas_call(functools.partial(exchange, rows, cols), out_shape=jax.Sha...  15.1 us
    div x1, other arithmetic, body(): return summed / scale[:, None]  1.67 us
    unnamed x2, local copies, waits for them, and re-layouts  0.68 us

profile of v1, /device:TPU:0, one launch (start us, length us, event | category | flops | bytes accessed | tf_op | source)
XLA Modules:
  0.0 17.5 jit_solution(5594969831915082896)
XLA Ops:
  0.0 0.0 copy-start
  0.0 0.7 %copy-done = s32[256]{0:T(256)S(1)} copy-done((s32[256]{0:T(256)S(1)}, s32[256]{0:T(256)}, u32[]{:S(2)}) %copy-start) | copy-done | bytes 1048
  0.7 15.1 %shard_map.46 = f32[256,128]{1,0:T(8,128)} custom-call(f32[32,16,128]{2,1,0:T(8,128)} %bitcast.4, s32[1,16,2,16]{3,2,1,0:T(2,128)} %dst_ref.1, s32[2,16]{1,0:T(2,128)} %bitcast.5), custom_call_target="tpu_custom_call" | custom-call | tf_op jit(solution)/shard_map/pallas_call | solution.py:111
  15.8 1.7 %broadcast_divide_fusion = f32[256,128]{1,0:T(8,128)} fusion(f32[256,128]{1,0:T(8,128)} %shard_map.46, f32[256]{0:T(256)S(1)} %maximum_convert_fusion), kind=kLoop, calls=%fused_computation | loop fusion | flops 32768 | bytes 263168 | tf_op jit(solution)/shard_map/div | solution.py:131
  (1 shorter events, 0.0 us)
Async XLA Ops:
  0.0 0.7 %copy-start = (s32[256]{0:T(256)S(1)}, s32[256]{0:T(256)}, u32[]{:S(2)}) copy-start(s32[256]{0:T(256)} %param.7) | copy-start | bytes 3076

commit v2 on v1

v2 whole, which is shorter than its diff:
```python
import functools

import jax
import jax.numpy as jnp
from jax import lax
from jax.experimental import pallas as pl
from jax.experimental.pallas import tpu as pltpu
from jax.sharding import PartitionSpec as P

MESH = pl.DeviceIdType.MESH
LANES = 128


def exchange(rows, cols, msg_ref, dst_ref, cnt_ref, out_ref, stage, recv, labels, dst, cnt, copy_sem, send_sem, recv_sem, up_sem):
    slots, width = msg_ref.shape[1:]
    owned = out_ref.shape[0]
    total = rows * cols
    pack = LANES // slots
    planes = total // pack
    me = lax.axis_index("row") * cols + lax.axis_index("col")
    plane, seat = me // pack, me % pack

    def device(t):
        return (t // cols, t % cols)

    def repeat(first, last, visit):
        if last - first <= 8:
            for i in range(first, last):
                visit(i)
        else:
            lax.fori_loop(first, last, lambda i, c: (visit(i), c)[1], 0)

    barrier = pltpu.get_barrier_semaphore()

    def greet(t):
        pl.semaphore_signal(barrier, inc=1, device_id=device(t), device_id_type=MESH)

    repeat(1, pack, lambda j: greet(plane * pack + (seat + j) % pack))
    has_below = plane > 0
    has_above = plane < planes - 1

    @pl.when(has_below)
    def _():
        greet(me - pack)

    @pl.when(has_above)
    def _():
        greet(me + pack)

    loads = [
        pltpu.make_async_copy(dst_ref, dst, copy_sem.at[0]),
        pltpu.make_async_copy(cnt_ref, cnt, copy_sem.at[1]),
        pltpu.make_async_copy(msg_ref, stage.at[:, pl.ds(0, slots), :], copy_sem.at[2]),
    ]
    for load in loads:
        load.start()
    labels[...] = jnp.zeros_like(labels)
    loads[0].wait()
    loads[1].wait()

    lane = lax.broadcasted_iota(jnp.int32, (cols, slots), 1)
    for g in range(rows):
        value = jnp.where(lane < cnt[:, g : g + 1], dst[0, g], -1)
        labels[pl.ds(g * cols, cols), pl.ds(0, slots)] = value.astype(jnp.float32)
    stage[:, slots, :] = pltpu.roll(labels[...], seat * slots, 1)
    loads[2].wait()

    def tell(q, t):
        pl.semaphore_signal(up_sem.at[q], inc=1, device_id=device(t), device_id_type=MESH)

    def send(t):
        pltpu.make_async_remote_copy(
            src_ref=stage.at[t],
            dst_ref=recv.at[me],
            send_sem=send_sem,
            recv_sem=recv_sem.at[plane],
            device_id=device(t),
            device_id_type=MESH,
        ).start()

    pl.semaphore_wait(barrier, pack + 1 - (planes - plane) // planes - (plane + 1) // planes)

    @pl.when(has_below)
    def _():
        tell(plane, me - pack)

    @pl.when(has_above)
    def _():
        tell(plane, me + pack)

    repeat(1, pack, lambda j: send(plane * pack + (seat + j) % pack))
    own = pltpu.make_async_copy(stage.at[me], recv.at[me], recv_sem.at[plane])
    own.start()

    def other(i):
        lower = (planes + plane - 1 - i) // planes
        return lower, lower * (plane - 1 - i) + (1 - lower) * (i + 1)

    def forward(i):
        lower, q = other(i)
        pl.semaphore_wait(up_sem.at[q], 1)
        onward = plane + 2 * lower - 1

        @pl.when((onward >= 0) & (onward < planes))
        def _():
            tell(q, onward * pack + seat)

        repeat(0, pack, lambda j: send(q * pack + (seat + j) % pack))

    repeat(0, planes - 1, forward)

    vertex = lax.broadcasted_iota(jnp.int32, (owned, LANES), 0).astype(jnp.float32)

    def block(q, acc):
        part = recv.at[pl.ds(q * pack, pack)]
        pltpu.make_async_copy(part, part, recv_sem.at[q]).wait()
        label = jnp.sum(recv[pl.ds(q * pack, pack), slots, :], axis=0, keepdims=True)
        hot = (vertex == label).astype(jnp.bfloat16)
        values = recv[pl.ds(q * pack, pack), pl.ds(0, slots), :].reshape(pack * slots, width)
        high = values.astype(jnp.bfloat16)
        low = (values - high.astype(jnp.float32)).astype(jnp.bfloat16)
        both = jnp.concatenate([high, low], axis=1)
        return acc + jnp.dot(hot, both, preferred_element_type=jnp.float32)

    acc = block(plane, jnp.zeros((owned, 2 * width), jnp.float32))
    if planes <= 8:
        for i in range(planes - 1):
            acc = block(other(i)[1], acc)
    else:
        acc = lax.fori_loop(0, planes - 1, lambda i, a: block(other(i)[1], a), acc)
    out_ref[...] = acc[:, :width] + acc[:, width:]
    sent = stage.at[pl.ds(0, total - 1)]
    pltpu.make_async_copy(sent, sent, send_sem).wait()


def solution(mesh):
    rows, cols = mesh.shape["row"], mesh.shape["col"]
    total = rows * cols

    def body(messages, dst_local, counts, degrees):
        slots, width = messages.shape[3:]
        owned = degrees.shape[0]
        planes = total // (LANES // slots)
        summed = pl.pallas_call(
            functools.partial(exchange, rows, cols),
            out_shape=jax.ShapeDtypeStruct((owned, width), jnp.float32),
            in_specs=[
                pl.BlockSpec(memory_space=pl.ANY),
                pl.BlockSpec(memory_space=pl.ANY),
                pl.BlockSpec(memory_space=pl.ANY),
            ],
            out_specs=pl.BlockSpec(memory_space=pltpu.VMEM),
            scratch_shapes=[
                pltpu.VMEM((total, slots + 1, width), jnp.float32),
                pltpu.VMEM((total, slots + 1, width), jnp.float32),
                pltpu.VMEM((total, LANES), jnp.float32),
                pltpu.VMEM(dst_local.shape, jnp.int32),
                pltpu.VMEM((cols, rows), jnp.int32),
                pltpu.SemaphoreType.DMA((3,)),
                pltpu.SemaphoreType.DMA,
                pltpu.SemaphoreType.DMA((planes,)),
                pltpu.SemaphoreType.REGULAR((planes,)),
            ],
            compiler_params=pltpu.CompilerParams(collective_id=0, has_side_effects=True),
        )(messages.reshape(total, slots, width), dst_local, counts[0].T)
        summed, degrees = lax.optimization_barrier((summed, degrees))
        scale = jnp.maximum(degrees, 1).astype(jnp.float32)
        return summed / scale[:, None]

    in_specs = (
        P(("row", "col"), None, None, None, None),
        P(("row", "col"), None, None, None),
        P(("row", "col"), None, None),
        P(("row", "col")),
    )
    return jax.shard_map(body, mesh=mesh, in_specs=in_specs, out_specs=P(("row", "col"), None), check_vma=False)
```

time: 17.7 us -> 16.5 us (0.932)
  local copies, waits for them, and re-layouts: 0.68 us -> 0.01 us
  Pallas kernels: 15.1 us -> 14.7 us
    unnamed x2, local copies, waits for them, and re-layouts: 0.68 us -> 0.01 us
    pallas_call x1, Pallas kernels: 15.1 us -> 14.7 us  [body(): pl.pallas_call(functools.partial(exchange, rows, cols), out_shape=jax.Sha...]
where the time goes in v2:
time: 16.5 us; the launch traced here: 16.4 us
  Pallas kernels  14.7 us (89%)
  other arithmetic  1.67 us (10%)
    pallas_call x1, Pallas kernels, body(): pl.pallas_call(functools.partial(exchange, rows, cols), out_shape=jax.Sha...  14.7 us
    div x1, other arithmetic, body(): return summed / scale[:, None]  1.67 us

profile of v2, /device:TPU:0, one launch (start us, length us, event | category | flops | bytes accessed | tf_op | source)
XLA Modules:
  0.0 16.4 jit_solution(2143434243975127649)
XLA Ops:
  0.0 0.0 copy-start
  0.0 14.7 %shard_map.46 = f32[256,128]{1,0:T(8,128)} custom-call(f32[32,16,128]{2,1,0:T(8,128)} %bitcast.4, s32[1,16,2,16]{3,2,1,0:T(2,128)} %dst_ref.1, s32[2,16]{1,0:T(2,128)} %bitcast.5), custom_call_target="tpu_custom_call" | custom-call | tf_op jit(solution)/shard_map/pallas_call | solution.py:144
  14.7 0.0 copy-done
  14.7 1.7 %broadcast_divide_fusion = f32[256,128]{1,0:T(8,128)} fusion(f32[256,128]{1,0:T(8,128)} %shard_map.46, f32[256]{0:T(256)S(1)} %maximum_convert_fusion), kind=kLoop, calls=%fused_computation | loop fusion | flops 32768 | bytes 263168 | tf_op jit(solution)/shard_map/div | solution.py:168
  (1 shorter events, 0.0 us)
Async XLA Ops:
  0.0 14.7 %copy-start = (s32[256]{0:T(256)S(1)}, s32[256]{0:T(256)}, u32[]{:S(2)}) copy-start(s32[256]{0:T(256)} %param.7) | copy-start | bytes 3076

commit v3 on v2

v3 whole, which is shorter than its diff:
```python
import functools

import jax
import jax.numpy as jnp
from jax import lax
from jax.experimental import pallas as pl
from jax.experimental.pallas import tpu as pltpu
from jax.sharding import PartitionSpec as P

MESH = pl.DeviceIdType.MESH
LANES = 128


def exchange(rows, cols, msg_ref, dst_ref, cnt_ref, deg_ref, out_ref, deg, stage, recv, labels, dst, cnt, copy_sem, send_sem, recv_sem, up_sem):
    slots, width = msg_ref.shape[1:]
    owned = out_ref.shape[0]
    total = rows * cols
    pack = LANES // slots
    planes = total // pack
    me = lax.axis_index("row") * cols + lax.axis_index("col")
    plane, seat = me // pack, me % pack

    def device(t):
        return (t // cols, t % cols)

    def repeat(first, last, visit):
        if last - first <= 8:
            for i in range(first, last):
                visit(i)
        else:
            lax.fori_loop(first, last, lambda i, c: (visit(i), c)[1], 0)

    loads = [
        pltpu.make_async_copy(dst_ref, dst, copy_sem.at[0]),
        pltpu.make_async_copy(cnt_ref, cnt, copy_sem.at[1]),
        pltpu.make_async_copy(deg_ref, deg, copy_sem.at[3]),
        pltpu.make_async_copy(msg_ref, stage.at[:, pl.ds(0, slots), :], copy_sem.at[2]),
    ]
    for load in loads:
        load.start()
    barrier = pltpu.get_barrier_semaphore()

    def greet(t):
        pl.semaphore_signal(barrier, inc=1, device_id=device(t), device_id_type=MESH)

    def greet_above(d):
        @pl.when(plane + d < planes)
        def _():
            repeat(0, pack, lambda j: greet((plane + d) * pack + (seat + j) % pack))

    repeat(1, pack, lambda j: greet(plane * pack + (seat + j) % pack))
    repeat(1, planes, greet_above)
    labels[...] = jnp.zeros_like(labels)
    loads[0].wait()
    loads[1].wait()

    lane = lax.broadcasted_iota(jnp.int32, (cols, slots), 1)
    for g in range(rows):
        value = jnp.where(lane < cnt[:, g : g + 1], dst[0, g], -1)
        labels[pl.ds(g * cols, cols), pl.ds(0, slots)] = value.astype(jnp.float32)
    stage[:, slots, :] = pltpu.roll(labels[...], seat * slots, 1)
    loads[2].wait()
    loads[3].wait()
    size = deg.shape[1]
    same = lax.broadcasted_iota(jnp.int32, (size, size), 0) == lax.broadcasted_iota(jnp.int32, (size, size), 1)
    scale = jnp.concatenate(
        [jnp.sum(jnp.where(same, jnp.maximum(deg[i : i + 1, :], 1), 0).astype(jnp.float32), axis=1, keepdims=True) for i in range(deg.shape[0])],
        axis=0,
    )

    def send(t):
        pltpu.make_async_remote_copy(
            src_ref=stage.at[t],
            dst_ref=recv.at[me],
            send_sem=send_sem,
            recv_sem=recv_sem.at[plane],
            device_id=device(t),
            device_id_type=MESH,
        ).start()

    pl.semaphore_wait(barrier, pack - 1 + pack * plane)

    def tell_below(d):
        @pl.when(plane - d >= 0)
        def _():
            t = me - d * pack
            pl.semaphore_signal(up_sem.at[plane], inc=1, device_id=device(t), device_id_type=MESH)

    def send_below(i):
        d = planes - i

        @pl.when(plane - d >= 0)
        def _():
            repeat(0, pack, lambda j: send((plane - d) * pack + j))

    def send_above(d):
        @pl.when(plane + d < planes)
        def _():
            pl.semaphore_wait(up_sem.at[plane + d], 1)
            repeat(0, pack, lambda j: send((plane + d) * pack + j))

    repeat(1, planes, tell_below)
    repeat(1, planes, send_below)
    repeat(1, pack, lambda j: send(plane * pack + (seat + j) % pack))
    own = pltpu.make_async_copy(stage.at[me], recv.at[me], recv_sem.at[plane])
    own.start()
    repeat(1, planes, send_above)

    def other(i):
        lower = (planes + plane - 1 - i) // planes
        return lower * (plane - 1 - i) + (1 - lower) * (i + 1)

    vertex = lax.broadcasted_iota(jnp.int32, (owned, LANES), 0).astype(jnp.float32)

    def block(q, acc):
        part = recv.at[pl.ds(q * pack, pack)]
        pltpu.make_async_copy(part, part, recv_sem.at[q]).wait()
        label = jnp.sum(recv[pl.ds(q * pack, pack), slots, :], axis=0, keepdims=True)
        hot = (vertex == label).astype(jnp.bfloat16)
        values = recv[pl.ds(q * pack, pack), pl.ds(0, slots), :].reshape(pack * slots, width)
        high = values.astype(jnp.bfloat16)
        low = (values - high.astype(jnp.float32)).astype(jnp.bfloat16)
        both = jnp.concatenate([high, low], axis=1)
        return acc + jnp.dot(hot, both, preferred_element_type=jnp.float32)

    acc = block(plane, jnp.zeros((owned, 2 * width), jnp.float32))
    if planes <= 8:
        for i in range(planes - 1):
            acc = block(other(i), acc)
    else:
        acc = lax.fori_loop(0, planes - 1, lambda i, a: block(other(i), a), acc)
    out_ref[...] = (acc[:, :width] + acc[:, width:]) / scale
    sent = stage.at[pl.ds(0, total - 1)]
    pltpu.make_async_copy(sent, sent, send_sem).wait()


def solution(mesh):
    rows, cols = mesh.shape["row"], mesh.shape["col"]
    total = rows * cols

    def body(messages, dst_local, counts, degrees):
        slots, width = messages.shape[3:]
        owned = degrees.shape[0]
        planes = total // (LANES // slots)
        summed = pl.pallas_call(
            functools.partial(exchange, rows, cols),
            out_shape=pltpu.VMEM((owned, width), jnp.float32),
            in_specs=[
                pl.BlockSpec(memory_space=pl.ANY),
                pl.BlockSpec(memory_space=pl.ANY),
                pl.BlockSpec(memory_space=pl.ANY),
                pl.BlockSpec(memory_space=pl.ANY),
            ],
            out_specs=pl.BlockSpec(memory_space=pltpu.VMEM),
            scratch_shapes=[
                pltpu.VMEM((owned // LANES, LANES), jnp.int32),
                pltpu.VMEM((total, slots + 1, width), jnp.float32),
                pltpu.VMEM((total, slots + 1, width), jnp.float32),
                pltpu.VMEM((total, LANES), jnp.float32),
                pltpu.VMEM(dst_local.shape, jnp.int32),
                pltpu.VMEM((cols, rows), jnp.int32),
                pltpu.SemaphoreType.DMA((4,)),
                pltpu.SemaphoreType.DMA,
                pltpu.SemaphoreType.DMA((planes,)),
                pltpu.SemaphoreType.REGULAR((planes,)),
            ],
            compiler_params=pltpu.CompilerParams(collective_id=0, has_side_effects=True),
        )(messages.reshape(total, slots, width), dst_local, counts[0].T, degrees.reshape(-1, LANES))
        return summed

    in_specs = (
        P(("row", "col"), None, None, None, None),
        P(("row", "col"), None, None, None),
        P(("row", "col"), None, None),
        P(("row", "col")),
    )
    return jax.shard_map(body, mesh=mesh, in_specs=in_specs, out_specs=P(("row", "col"), None), check_vma=False)
```

time: 16.5 us -> 12.5 us (0.76)
  the two profiles are of different devices: /device:TPU:0 before, /device:TPU:31 now
where the time goes in v3:
time: 12.5 us; the launch traced here: 12.3 us
  Pallas kernels  11.6 us (93%)
  local copies, waits for them, and re-layouts  0.66 us (5%)
    pallas_call x1, Pallas kernels, body(): pl.pallas_call(functools.partial(exchange, rows, cols), out_shape=pltpu.V...  11.6 us
    unnamed x1, local copies, waits for them, and re-layouts  0.66 us

profile of v3, /device:TPU:31, one launch (start us, length us, event | category | flops | bytes accessed | tf_op | source)
XLA Modules:
  0.0 12.3 jit_solution(15183485389512986127)
XLA Ops:
  0.0 11.6 %shard_map.46 = f32[256,128]{1,0:T(8,128)S(1)} custom-call(f32[32,16,128]{2,1,0:T(8,128)} %bitcast.5, s32[1,16,2,16]{3,2,1,0:T(2,128)} %dst_ref.1, s32[2,16]{1,0:T(2,128)} %bitcast.6, s32[2,128]{1,0:T(2,128)} %bitcast.7), custom_call_target="tpu_custom_call" | custom-call | tf_op jit(solution)/shard_map/pallas_call | solution.py:145
  11.6 0.7 %copy.6 = f32[256,128]{1,0:T(8,128)} copy(f32[256,128]{1,0:T(8,128)S(1)} %shard_map.46) | data formatting | bytes 262144

commit v4 on v3

--- a/solution.py
+++ b/solution.py
@@ -11,7 +11,7 @@
 LANES = 128
 
 
-def exchange(rows, cols, msg_ref, dst_ref, cnt_ref, deg_ref, out_ref, deg, stage, recv, labels, dst, cnt, copy_sem, send_sem, recv_sem, up_sem):
+def exchange(rows, cols, msg_ref, dst_ref, cnt_ref, deg_ref, out_ref, deg, stage, recv, labels, dst, cnt, spare, copy_sem, send_sem, recv_sem, up_sem, extra_sem, pass_sem, tail_sem):
     slots, width = msg_ref.shape[1:]
     owned = out_ref.shape[0]
     total = rows * cols
@@ -19,6 +19,10 @@
     planes = total // pack
     me = lax.axis_index("row") * cols + lax.axis_index("col")
     plane, seat = me // pack, me % pack
+    core = lax.axis_index("col")
+    paired = cols == 2 and slots % 16 == 0
+    cut = slots // 2 if paired else 0
+    pairs = pack // cols
 
     def device(t):
         return (t // cols, t % cols)
@@ -34,8 +38,10 @@
         pltpu.make_async_copy(dst_ref, dst, copy_sem.at[0]),
         pltpu.make_async_copy(cnt_ref, cnt, copy_sem.at[1]),
         pltpu.make_async_copy(deg_ref, deg, copy_sem.at[3]),
-        pltpu.make_async_copy(msg_ref, stage.at[:, pl.ds(0, slots), :], copy_sem.at[2]),
+        pltpu.make_async_copy(msg_ref.at[:, pl.ds(0, slots - cut)], stage.at[:, pl.ds(cut, slots - cut), :], copy_sem.at[2]),
     ]
+    if paired:
+        loads.append(pltpu.make_async_copy(msg_ref.at[:, pl.ds(cut, cut)], spare, copy_sem.at[4]))
     for load in loads:
         load.start()
     barrier = pltpu.get_barrier_semaphore()
@@ -55,12 +61,24 @@
     loads[1].wait()
 
     lane = lax.broadcasted_iota(jnp.int32, (cols, slots), 1)
+    base = lax.broadcasted_iota(jnp.int32, (cols, slots), 0) * owned
     for g in range(rows):
-        value = jnp.where(lane < cnt[:, g : g + 1], dst[0, g], -1)
-        labels[pl.ds(g * cols, cols), pl.ds(0, slots)] = value.astype(jnp.float32)
+        value = jnp.where(lane < cnt[:, g : g + 1], dst[0, g] + base, -1).astype(jnp.float32)
+        if paired:
+            second = cnt[1:2, g : g + 1] > cnt[0:1, g : g + 1]
+            extra = jnp.where(second, value[1:2, cut:], value[0:1, cut:])
+            labels[pl.ds(g * cols, cols), pl.ds(0, cut)] = jnp.broadcast_to(extra, (cols, cut))
+            labels[pl.ds(g * cols, cols), pl.ds(cut, cut)] = value[:, :cut]
+        else:
+            labels[pl.ds(g * cols, cols), pl.ds(0, slots)] = value
     stage[:, slots, :] = pltpu.roll(labels[...], seat * slots, 1)
     loads[2].wait()
     loads[3].wait()
+    if paired:
+        loads[4].wait()
+        for g in range(rows):
+            second = cnt[1:2, g : g + 1] > cnt[0:1, g : g + 1]
+            stage[g, pl.ds(0, cut), :] = jnp.where(second, spare[g * cols + 1], spare[g * cols])
     size = deg.shape[1]
     same = lax.broadcasted_iota(jnp.int32, (size, size), 0) == lax.broadcasted_iota(jnp.int32, (size, size), 1)
     scale = jnp.concatenate(
@@ -68,16 +86,34 @@
         axis=0,
     )
 
+    body = pl.ds(cut, slots + 1 - cut)
+    head = pl.ds(0, cut)
+
     def send(t):
         pltpu.make_async_remote_copy(
-            src_ref=stage.at[t],
-            dst_ref=recv.at[me],
+            src_ref=stage.at[t, body],
+            dst_ref=recv.at[me // cols, core, body],
             send_sem=send_sem,
             recv_sem=recv_sem.at[plane],
             device_id=device(t),
             device_id_type=MESH,
         ).start()
 
+    def send_extra(g):
+        pltpu.make_async_remote_copy(
+            src_ref=stage.at[g, head],
+            dst_ref=recv.at[me // cols, core, head],
+            send_sem=tail_sem.at[0],
+            recv_sem=extra_sem.at[plane],
+            device_id=(g, core),
+            device_id_type=MESH,
+        ).start()
+
+    def send_plane(q):
+        if paired:
+            repeat(0, pairs, lambda j: send_extra(q * pairs + j))
+        repeat(0, pack, lambda j: send(q * pack + j))
+
     pl.semaphore_wait(barrier, pack - 1 + pack * plane)
 
     def tell_below(d):
@@ -91,33 +127,54 @@
 
         @pl.when(plane - d >= 0)
         def _():
-            repeat(0, pack, lambda j: send((plane - d) * pack + j))
+            send_plane(plane - d)
 
     def send_above(d):
         @pl.when(plane + d < planes)
         def _():
             pl.semaphore_wait(up_sem.at[plane + d], 1)
-            repeat(0, pack, lambda j: send((plane + d) * pack + j))
+            send_plane(plane + d)
 
     repeat(1, planes, tell_below)
     repeat(1, planes, send_below)
+    if paired:
+        repeat(1, pairs, lambda j: send_extra(plane * pairs + (seat // cols + j) % pairs))
+        pltpu.make_async_copy(stage.at[me // cols, head], recv.at[me // cols, core, head], extra_sem.at[plane]).start()
     repeat(1, pack, lambda j: send(plane * pack + (seat + j) % pack))
-    own = pltpu.make_async_copy(stage.at[me], recv.at[me], recv_sem.at[plane])
-    own.start()
+    pltpu.make_async_copy(stage.at[me, body], recv.at[me // cols, core, body], recv_sem.at[plane]).start()
     repeat(1, planes, send_above)
 
     def other(i):
         lower = (planes + plane - 1 - i) // planes
         return lower * (plane - 1 - i) + (1 - lower) * (i + 1)
 
-    vertex = lax.broadcasted_iota(jnp.int32, (owned, LANES), 0).astype(jnp.float32)
+    def hand(q):
+        part = recv.at[pl.ds(q * pairs, pairs), core, head]
+        pltpu.make_async_copy(part, part, extra_sem.at[q]).wait()
+        pltpu.make_async_remote_copy(
+            src_ref=part,
+            dst_ref=part,
+            send_sem=tail_sem.at[1],
+            recv_sem=pass_sem.at[q],
+            device_id=(lax.axis_index("row"), 1 - core),
+            device_id_type=MESH,
+        ).start()
+
+    if paired:
+        hand(plane)
+        repeat(0, planes - 1, lambda i: hand(other(i)))
+
+    vertex = (lax.broadcasted_iota(jnp.int32, (owned, LANES), 0) + core * owned).astype(jnp.float32)
 
     def block(q, acc):
-        part = recv.at[pl.ds(q * pack, pack)]
+        part = recv.at[pl.ds(q * pairs, pairs), :, body]
         pltpu.make_async_copy(part, part, recv_sem.at[q]).wait()
-        label = jnp.sum(recv[pl.ds(q * pack, pack), slots, :], axis=0, keepdims=True)
+        if paired:
+            part = recv.at[pl.ds(q * pairs, pairs), 1 - core, head]
+            pltpu.make_async_copy(part, part, pass_sem.at[q]).wait()
+        label = jnp.sum(recv[pl.ds(q * pairs, pairs), :, slots, :].reshape(pack, width), axis=0, keepdims=True)
         hot = (vertex == label).astype(jnp.bfloat16)
-        values = recv[pl.ds(q * pack, pack), pl.ds(0, slots), :].reshape(pack * slots, width)
+        values = recv[pl.ds(q * pairs, pairs), :, pl.ds(0, slots), :].reshape(pack * slots, width)
         high = values.astype(jnp.bfloat16)
         low = (values - high.astype(jnp.float32)).astype(jnp.bfloat16)
         both = jnp.concatenate([high, low], axis=1)
@@ -130,8 +187,12 @@
     else:
         acc = lax.fori_loop(0, planes - 1, lambda i, a: block(other(i), a), acc)
     out_ref[...] = (acc[:, :width] + acc[:, width:]) / scale
-    sent = stage.at[pl.ds(0, total - 1)]
+    sent = stage.at[pl.ds(0, total - 1), body]
     pltpu.make_async_copy(sent, sent, send_sem).wait()
+    if paired:
+        for count, sem in ((rows - 1, 0), (rows, 1)):
+            sent = stage.at[pl.ds(0, count), head]
+            pltpu.make_async_copy(sent, sent, tail_sem.at[sem]).wait()
 
 
 def solution(mesh):
@@ -155,14 +216,18 @@
             scratch_shapes=[
                 pltpu.VMEM((owned // LANES, LANES), jnp.int32),
                 pltpu.VMEM((total, slots + 1, width), jnp.float32),
-                pltpu.VMEM((total, slots + 1, width), jnp.float32),
+                pltpu.VMEM((rows, cols, slots + 1, width), jnp.float32),
                 pltpu.VMEM((total, LANES), jnp.float32),
                 pltpu.VMEM(dst_local.shape, jnp.int32),
                 pltpu.VMEM((cols, rows), jnp.int32),
-                pltpu.SemaphoreType.DMA((4,)),
+                pltpu.VMEM((total, slots // 2, width), jnp.float32),
+                pltpu.SemaphoreType.DMA((5,)),
                 pltpu.SemaphoreType.DMA,
                 pltpu.SemaphoreType.DMA((planes,)),
                 pltpu.SemaphoreType.REGULAR((planes,)),
+                pltpu.SemaphoreType.DMA((planes,)),
+                pltpu.SemaphoreType.DMA((planes,)),
+                pltpu.SemaphoreType.DMA((2,)),
             ],
             compiler_params=pltpu.CompilerParams(collective_id=0, has_side_effects=True),
         )(messages.reshape(total, slots, width), dst_local, counts[0].T, degrees.reshape(-1, LANES))

time: 12.5 us -> 12.5 us (level)
  the two profiles are of different devices: /device:TPU:31 before, /device:TPU:25 now
where the time goes in v4:
time: 12.5 us; the launch traced here: 12.3 us
  Pallas kernels  11.6 us (93%)
  local copies, waits for them, and re-layouts  0.66 us (5%)
    pallas_call x1, Pallas kernels, body(): pl.pallas_call(functools.partial(exchange, rows, cols), out_shape=pltpu.V...  11.6 us
    unnamed x1, local copies, waits for them, and re-layouts  0.66 us

profile of v4, /device:TPU:25, one launch (start us, length us, event | category | flops | bytes accessed | tf_op | source)
XLA Modules:
  0.0 12.3 jit_solution(11734438580788273187)
XLA Ops:
  0.0 11.6 %shard_map.46 = f32[256,128]{1,0:T(8,128)S(1)} custom-call(f32[32,16,128]{2,1,0:T(8,128)} %bitcast.5, s32[1,16,2,16]{3,2,1,0:T(2,128)} %dst_ref.1, s32[2,16]{1,0:T(2,128)} %bitcast.6, s32[2,128]{1,0:T(2,128)} %bitcast.7), custom_call_target="tpu_custom_call" | custom-call | tf_op jit(solution)/shard_map/pallas_call | solution.py:206
  11.6 0.7 %copy.6 = f32[256,128]{1,0:T(8,128)} copy(f32[256,128]{1,0:T(8,128)S(1)} %shard_map.46) | data formatting | bytes 262144

commit v5 on v4

--- a/solution.py
+++ b/solution.py
@@ -105,7 +105,7 @@
             dst_ref=recv.at[me // cols, core, head],
             send_sem=tail_sem.at[0],
             recv_sem=extra_sem.at[plane],
-            device_id=(g, core),
+            device_id=(g, 1 - core),
             device_id_type=MESH,
         ).start()
 
@@ -138,8 +138,7 @@
     repeat(1, planes, tell_below)
     repeat(1, planes, send_below)
     if paired:
-        repeat(1, pairs, lambda j: send_extra(plane * pairs + (seat // cols + j) % pairs))
-        pltpu.make_async_copy(stage.at[me // cols, head], recv.at[me // cols, core, head], extra_sem.at[plane]).start()
+        repeat(0, pairs, lambda j: send_extra(plane * pairs + (seat // cols + j) % pairs))
     repeat(1, pack, lambda j: send(plane * pack + (seat + j) % pack))
     pltpu.make_async_copy(stage.at[me, body], recv.at[me // cols, core, body], recv_sem.at[plane]).start()
     repeat(1, planes, send_above)
@@ -149,7 +148,7 @@
         return lower * (plane - 1 - i) + (1 - lower) * (i + 1)
 
     def hand(q):
-        part = recv.at[pl.ds(q * pairs, pairs), core, head]
+        part = recv.at[pl.ds(q * pairs, pairs), 1 - core, head]
         pltpu.make_async_copy(part, part, extra_sem.at[q]).wait()
         pltpu.make_async_remote_copy(
             src_ref=part,
@@ -170,7 +169,7 @@
         part = recv.at[pl.ds(q * pairs, pairs), :, body]
         pltpu.make_async_copy(part, part, recv_sem.at[q]).wait()
         if paired:
-            part = recv.at[pl.ds(q * pairs, pairs), 1 - core, head]
+            part = recv.at[pl.ds(q * pairs, pairs), core, head]
             pltpu.make_async_copy(part, part, pass_sem.at[q]).wait()
         label = jnp.sum(recv[pl.ds(q * pairs, pairs), :, slots, :].reshape(pack, width), axis=0, keepdims=True)
         hot = (vertex == label).astype(jnp.bfloat16)
@@ -190,7 +189,7 @@
     sent = stage.at[pl.ds(0, total - 1), body]
     pltpu.make_async_copy(sent, sent, send_sem).wait()
     if paired:
-        for count, sem in ((rows - 1, 0), (rows, 1)):
+        for count, sem in ((rows, 0), (rows, 1)):
             sent = stage.at[pl.ds(0, count), head]
             pltpu.make_async_copy(sent, sent, tail_sem.at[sem]).wait()
 

time: 12.5 us -> 12.2 us (0.976)
  the two profiles are of different devices: /device:TPU:25 before, /device:TPU:0 now
where the time goes in v5:
time: 12.2 us; the launch traced here: 12 us
  Pallas kernels  11.3 us (93%)
  local copies, waits for them, and re-layouts  0.66 us (5%)
    pallas_call x1, Pallas kernels, body(): pl.pallas_call(functools.partial(exchange, rows, cols), out_shape=pltpu.V...  11.3 us
    unnamed x1, local copies, waits for them, and re-layouts  0.66 us

profile of v5, /device:TPU:0, one launch (start us, length us, event | category | flops | bytes accessed | tf_op | source)
XLA Modules:
  0.0 12.0 jit_solution(18104032828528868163)
XLA Ops:
  0.0 11.3 %shard_map.46 = f32[256,128]{1,0:T(8,128)S(1)} custom-call(f32[32,16,128]{2,1,0:T(8,128)} %bitcast.5, s32[1,16,2,16]{3,2,1,0:T(2,128)} %dst_ref.1, s32[2,16]{1,0:T(2,128)} %bitcast.6, s32[2,128]{1,0:T(2,128)} %bitcast.7), custom_call_target="tpu_custom_call" | custom-call | tf_op jit(solution)/shard_map/pallas_call | solution.py:205
  11.3 0.7 %copy.6 = f32[256,128]{1,0:T(8,128)} copy(f32[256,128]{1,0:T(8,128)S(1)} %shard_map.46) | data formatting | bytes 262144

commit v6 on v5

--- a/solution.py
+++ b/solution.py
@@ -110,9 +110,13 @@
         ).start()
 
     def send_plane(q):
-        if paired:
-            repeat(0, pairs, lambda j: send_extra(q * pairs + j))
-        repeat(0, pack, lambda j: send(q * pack + j))
+        def send_chip(j):
+            if paired:
+                send_extra(q * pairs + j)
+            for c in range(cols):
+                send(q * pack + j * cols + c)
+
+        repeat(0, pairs, send_chip)
 
     pl.semaphore_wait(barrier, pack - 1 + pack * plane)
 

time: 12.2 us -> 11.9 us (0.975)
  the two profiles are of different devices: /device:TPU:0 before, /device:TPU:31 now
where the time goes in v6:
time: 11.9 us; the launch traced here: 11.7 us
  Pallas kernels  11 us (92%)
  local copies, waits for them, and re-layouts  0.66 us (6%)
    pallas_call x1, Pallas kernels, body(): pl.pallas_call(functools.partial(exchange, rows, cols), out_shape=pltpu.V...  11 us
    unnamed x1, local copies, waits for them, and re-layouts  0.66 us

profile of v6, /device:TPU:31, one launch (start us, length us, event | category | flops | bytes accessed | tf_op | source)
XLA Modules:
  0.0 11.7 jit_solution(1010029700240305464)
XLA Ops:
  0.0 11.0 %shard_map.46 = f32[256,128]{1,0:T(8,128)S(1)} custom-call(f32[32,16,128]{2,1,0:T(8,128)} %bitcast.5, s32[1,16,2,16]{3,2,1,0:T(2,128)} %dst_ref.1, s32[2,16]{1,0:T(2,128)} %bitcast.6, s32[2,128]{1,0:T(2,128)} %bitcast.7), custom_call_target="tpu_custom_call" | custom-call | tf_op jit(solution)/shard_map/pallas_call | solution.py:209
  11.0 0.7 %copy.6 = f32[256,128]{1,0:T(8,128)} copy(f32[256,128]{1,0:T(8,128)S(1)} %shard_map.46) | data formatting | bytes 262144
